TPU v7x, 256 devices: a whole 4x4x8 slice. The times are simulated.
256 devices in a mesh: dp: 32 (over z, x_hi, core), owner: 8 (over x_lo, y).
Axes of the slice: x: 4 (x_hi: 2, x_lo: 2; x = x_hi * 2 + x_lo), y: 4, z: 8, core: 2. Of those that a mesh axis runs over, the one named last changes fastest.
Arguments:
- edge_in: bfloat16 [8, 65536, 512], P(None, ('dp', 'owner')), may hold values from -256 to 256
- edge_grad: bfloat16 [8, 65536, 512], P(None, ('dp', 'owner')), may hold values from -1.1953125 to 1.1953125
- row_mask: int32 [8, 65536], P(None, ('dp', 'owner')), may hold values 0 or 1
- layer_at: int32 [8], replicated, may hold values from 0 to 7, each once
Outputs:
- update: bfloat16 [8, 512, 512], P('owner')
Inputs may be any that keep to these rules, and one draw needn't show every extreme that they name: `layer_at`: every layer number appears once.
All inputs are finite; a program needn't handle non-finite values. No bound on the sum of `row_mask` on one device may be relied on, other than what follows from the above.
Results may differ from a plain program's by a relative error of at most 0.0085.
Values may be sent and summed in bfloat16 or wider, within the bound.
No kernel may reach another device: no remote copies, remote signals or barrier semaphores. Data moves between devices by JAX's collectives and lax.ppermute only.
A program may use at most 64 MiB of HBM per device.

v0:
```python
import math

import jax
import jax.numpy as jnp
from jax import lax
from jax.experimental import pallas as pl
from jax.experimental.pallas import tpu as pltpu
from jax.sharding import Mesh
from jax.sharding import PartitionSpec as P

ITERS = 4
DP = ("dp_0", "dp_1", "dp_2")
DP_OWNER = ("dp_0", "dp_1", "dp_2", "owner")
MASK_ROWS = 8
TILE = 128


def upper_tiles(count):
    return [(i, j) for i in range(count) for j in range(i, count)]


def pack_kernel(at_ref, in_ref, grad_ref, mask_ref, out_ref):
    rows = in_ref.shape[1]
    width = in_ref.shape[2]
    out_ref[0, :rows, :] = in_ref[0]
    out_ref[0, rows : 2 * rows, :] = grad_ref[0]
    line = mask_ref[pl.ds(at_ref[pl.program_id(0)], 1), :].astype(jnp.float32)
    spare = jnp.zeros((MASK_ROWS, width - rows), jnp.float32)
    wide = jnp.concatenate([jnp.broadcast_to(line, (MASK_ROWS, rows)), spare], axis=1)
    out_ref[0, 2 * rows :, :] = wide.astype(jnp.bfloat16)


def pack(edge_in, edge_grad, row_mask, layer_at):
    layers, rows, width = edge_in.shape
    lines = 2 * rows + MASK_ROWS
    return pl.pallas_call(
        pack_kernel,
        out_shape=jax.ShapeDtypeStruct((layers, lines, width), jnp.bfloat16),
        grid_spec=pltpu.PrefetchScalarGridSpec(
            num_scalar_prefetch=1,
            grid=(layers,),
            in_specs=[
                pl.BlockSpec((1, rows, width), lambda s, at: (at[s], 0, 0)),
                pl.BlockSpec((1, rows, width), lambda s, at: (at[s], 0, 0)),
                pl.BlockSpec((layers, rows), lambda s, at: (0, 0)),
            ],
            out_specs=pl.BlockSpec((1, lines, width), lambda s, at: (s, 0, 0)),
        ),
    )(layer_at, edge_in, edge_grad, row_mask)


def gram_kernel(scale_factor, scale_grad, rows, held_ref, out_ref, in_acc, out_acc, grad_acc):
    step = pl.program_id(0)
    inputs = jnp.concatenate([held_ref[k, :rows, :] for k in range(held_ref.shape[0])], axis=0)
    grads = jnp.concatenate(
        [held_ref[k, rows : 2 * rows, :] for k in range(held_ref.shape[0])], axis=0
    )
    weights = jnp.concatenate(
        [held_ref[k, 2 * rows : 2 * rows + 1, :rows] for k in range(held_ref.shape[0])], axis=1
    )
    in_turned = inputs.T
    grad_turned = grads.T
    term_in = jnp.dot(in_turned * weights, inputs, preferred_element_type=jnp.float32)
    term_out = jnp.dot(grad_turned * weights, grads, preferred_element_type=jnp.float32)
    term_grad = jnp.dot(in_turned, grads, preferred_element_type=jnp.float32)

    @pl.when(step == 0)
    def _():
        in_acc[...] = term_in
        out_acc[...] = term_out
        grad_acc[...] = term_grad

    @pl.when(step > 0)
    def _():
        in_acc[...] += term_in
        out_acc[...] += term_out
        grad_acc[...] += term_grad

    @pl.when(step == pl.num_programs(0) - 1)
    def _():
        count = in_acc.shape[0] // TILE
        spot = 0
        for acc, scale, tiles in (
            (in_acc, scale_factor, upper_tiles(count)),
            (out_acc, scale_factor, upper_tiles(count)),
            (grad_acc, scale_grad, [(i, j) for i in range(count) for j in range(count)]),
        ):
            for i, j in tiles:
                tile = acc[i * TILE : (i + 1) * TILE, j * TILE : (j + 1) * TILE] * scale
                out_ref[spot : spot + TILE, :] = tile.astype(jnp.bfloat16)
                spot += TILE


def packed_lines(width):
    count = width // TILE
    return (count * (count + 1) + count * count) * TILE


def gram(held, rows, width, rows_all):
    sources, lines, _ = held.shape
    many = 2
    kernel = lambda *refs: gram_kernel(1.0 / rows_all, 1.0 / math.sqrt(rows_all), rows, *refs)
    return pl.pallas_call(
        kernel,
        name="gram",
        out_shape=jax.ShapeDtypeStruct((packed_lines(width), TILE), jnp.bfloat16),
        grid=(sources // many,),
        in_specs=[pl.BlockSpec((many, lines, width), lambda s: (s, 0, 0))],
        out_specs=pl.BlockSpec((packed_lines(width), TILE), lambda s: (0, 0)),
        scratch_shapes=[pltpu.VMEM((width, width), jnp.float32)] * 3,
    )(held)


def total_kernel(arrived_ref, copies_ref):
    whole = arrived_ref[0].astype(jnp.float32)
    for k in range(1, arrived_ref.shape[0]):
        whole += arrived_ref[k].astype(jnp.float32)
    low = whole.astype(jnp.bfloat16)
    for k in range(copies_ref.shape[0]):
        copies_ref[k] = low


def total_copies(arrived):
    return pl.pallas_call(
        total_kernel,
        name="total",
        out_shape=jax.ShapeDtypeStruct(arrived.shape, arrived.dtype),
        in_specs=[pl.BlockSpec(memory_space=pltpu.VMEM)],
        out_specs=pl.BlockSpec(memory_space=pltpu.VMEM),
    )(arrived)


def newton_kernel(width, packed_ref, out_ref, in_ref, grad_out_ref, mid_ref):
    count = width // TILE
    tiles = upper_tiles(count)
    diagonal = (
        lax.broadcasted_iota(jnp.int32, (TILE, TILE), 0)
        == lax.broadcasted_iota(jnp.int32, (TILE, TILE), 1)
    )
    starts = []
    for ref, base in ((in_ref, 0), (grad_out_ref, len(tiles) * TILE)):
        trace = jnp.float32(0.0)
        for k, (i, j) in enumerate(tiles):
            tile = packed_ref[base + k * TILE : base + (k + 1) * TILE, :].astype(jnp.float32)
            ref[i * TILE : (i + 1) * TILE, j * TILE : (j + 1) * TILE] = tile
            if i == j:
                trace += jnp.sum(jnp.where(diagonal, tile, 0.0))
            else:
                ref[j * TILE : (j + 1) * TILE, i * TILE : (i + 1) * TILE] = tile.T
        shift = jnp.where(diagonal, trace * (0.05 / width), 0.0)
        for i in range(count):
            at = slice(i * TILE, (i + 1) * TILE)
            ref[at, at] += shift
        whole = ref[...]
        scale = lax.rsqrt(jnp.sum(whole * whole) + 1e-06)
        ref[...] = whole * scale
        starts.append(scale)
    base = 2 * len(tiles) * TILE
    for i in range(count):
        for j in range(count):
            k = base + (i * count + j) * TILE
            mid_ref[i * TILE : (i + 1) * TILE, j * TILE : (j + 1) * TILE] = packed_ref[
                k : k + TILE, :
            ].astype(jnp.float32)

    def dot(a, b):
        return jnp.dot(a, b, preferred_element_type=jnp.float32)

    for step in range(ITERS):
        left = in_ref[...]
        right = grad_out_ref[...]
        left_low = left.astype(jnp.bfloat16)
        right_low = right.astype(jnp.bfloat16)
        mid = mid_ref[...]
        mid = 2.0 * mid - dot(left_low, mid.astype(jnp.bfloat16))
        mid = 2.0 * mid - dot(mid.astype(jnp.bfloat16), right_low)
        if step < ITERS - 1:
            mid_ref[...] = mid
            in_ref[...] = 2.0 * left - dot(left_low, left_low)
            grad_out_ref[...] = 2.0 * right - dot(right_low, right_low)
        else:
            out_ref[...] = (mid * starts[0] * starts[1]).astype(jnp.bfloat16)


def newton(packed, width):
    return pl.pallas_call(
        lambda *refs: newton_kernel(width, *refs),
        name="newton",
        out_shape=jax.ShapeDtypeStruct((width, width), jnp.bfloat16),
        in_specs=[pl.BlockSpec(memory_space=pltpu.VMEM)],
        out_specs=pl.BlockSpec(memory_space=pltpu.VMEM),
        scratch_shapes=[pltpu.VMEM((width, width), jnp.float32)] * 3,
    )(packed)


def local(edge_in, edge_grad, row_mask, layer_at):
    rows = edge_in.shape[1]
    width = edge_in.shape[2]
    replicas = lax.axis_size(DP)
    rows_all = rows * replicas * lax.axis_size("owner")
    sent = pack(edge_in, edge_grad, row_mask, layer_at)
    held = lax.all_to_all(sent, "owner", 0, 0, tiled=True)
    partial = gram(held, rows, width, rows_all)
    pieces = partial.reshape(replicas, -1, TILE)
    arrived = lax.all_to_all(pieces, DP, 0, 0, tiled=True)
    whole = lax.all_to_all(total_copies(arrived), DP, 0, 0, tiled=True)
    update = newton(whole.reshape(-1, TILE), width)
    return update[None]


def solution(mesh):
    split = Mesh(
        mesh.devices.reshape(8, 2, 2, mesh.shape["owner"]), ("dp_0", "dp_1", "dp_2", "owner")
    )
    placed = (P(None, DP_OWNER, None), P(None, DP_OWNER, None), P(None, DP_OWNER), P())
    return jax.shard_map(
        local, mesh=split, in_specs=placed, out_specs=P("owner", None, None), check_vma=False
    )
```

profile of v0, /device:TPU:1, one launch (start us, length us, event | category | flops | bytes accessed | tf_op | source)
XLA Modules:
  0.0 164.2 jit_solution(5636826843432872351)
XLA Ops:
  0.0 7.3 %shard_map.46 = bf16[8,520,512]{2,1,0:T(8,128)(2,1)} custom-call(s32[8]{0:T(128)} %at_ref.1, bf16[8,256,512]{2,1,0:T(8,128)(2,1)} %in_ref.1, bf16[8,256,512]{2,1,0:T(8,128)(2,1)} %grad_ref.1, s32[8,256]{1,0:T(8,128)} %mask_ref.1), custom_call_target="tpu_custom_call" | custom-call | tf_op jit(solution)/shard_map/pallas_call | solution.py:36
  7.3 54.4 %all_to_all.15.refs_0_ = bf16[8,520,512]{2,1,0:T(8,128)(2,1)} all-to-all(bf16[8,520,512]{2,1,0:T(8,128)(2,1)} %shard_map.46), channel_id=1, replica_groups=mesh['dp_0'=8,'dp_1'=2,'dp_2'=2,'owner'=8] {'owner'}, dimensions={0} | all-to-all | bytes 8519680 | tf_op jit(solution)/shard_map/all_to_all | solution.py:202
  61.8 7.6 %gram.1 = bf16[4608,128]{1,0:T(8,128)(2,1)} custom-call(bf16[8,520,512]{2,1,0:T(8,128)(2,1)} %all_to_all.15.refs_0_), custom_call_target="tpu_custom_call" | custom-call | tf_op jit(solution)/shard_map/gram/pallas_call | solution.py:103
  69.4 47.1 %all_to_all.16.arrived_ref = bf16[32,144,128]{2,1,0:T(8,128)(2,1)} all-to-all(bf16[32,144,128]{2,1,0:T(8,128)(2,1)} %bitcast.4), channel_id=1, replica_groups=mesh['dp_0'=8,'dp_1'=2,'dp_2'=2,'owner'=8] {'dp_0','dp_1','dp_2'}, dimensions={0} | all-to-all | bytes 2359296 | tf_op jit(solution)/shard_map/all_to_all | solution.py:205
  116.5 2.5 %total.1 = bf16[32,144,128]{2,1,0:T(8,128)(2,1)} custom-call(bf16[32,144,128]{2,1,0:T(8,128)(2,1)} %all_to_all.16.arrived_ref), custom_call_target="tpu_custom_call" | custom-call | tf_op jit(solution)/shard_map/total/pallas_call | solution.py:124
  119.0 38.2 %all_to_all.17 = bf16[32,144,128]{2,1,0:T(8,128)(2,1)} all-to-all(bf16[32,144,128]{2,1,0:T(8,128)(2,1)} %total.1), channel_id=1, replica_groups=mesh['dp_0'=8,'dp_1'=2,'dp_2'=2,'owner'=8] {'dp_0','dp_1','dp_2'}, dimensions={0} | all-to-all | bytes 2359296 | tf_op jit(solution)/shard_map/all_to_all | solution.py:206
  157.2 7.0 %newton.1 = bf16[512,512]{1,0:T(8,128)(2,1)} custom-call(bf16[4608,128]{1,0:T(8,128)(2,1)} %bitcast.3), custom_call_target="tpu_custom_call" | custom-call | tf_op jit(solution)/shard_map/newton/pallas_call | solution.py:186
where the time goes:
time: 165 us; the launch traced here: 164 us
  blocking collectives  140 us (85%)
  Pallas kernels  24.5 us (15%)
    all_to_all x1, blocking collectives, local(): held = lax.all_to_all(sent, 'owner', 0, 0, tiled=True)  54.4 us
    all_to_all x1, blocking collectives, local(): arrived = lax.all_to_all(pieces, DP, 0, 0, tiled=True)  47.1 us
    all_to_all x1, blocking collectives, local(): whole = lax.all_to_all(total_copies(arrived), DP, 0, 0, tiled=True)  38.2 us
    pallas_call x1, Pallas kernels, gram(): pl.pallas_call(kernel, name='gram', out_shape=jax.ShapeDtypeStruct((packe...  7.6 us
    pallas_call x1, Pallas kernels, pack(): pl.pallas_call(pack_kernel, out_shape=jax.ShapeDtypeStruct((layers, lines...  7.33 us
    pallas_call x1, Pallas kernels, newton(): pl.pallas_call(lambda *refs: newton_kernel(width, *refs), name='newton',...  7.02 us

commit v1 on v0

v1 whole, which is shorter than its diff:
```python
import math

import jax
import jax.numpy as jnp
from jax import lax
from jax.experimental import pallas as pl
from jax.experimental.pallas import tpu as pltpu
from jax.sharding import Mesh
from jax.sharding import PartitionSpec as P

ITERS = 4
DP = ("dp_0", "dp_1", "dp_2")
DP_OWNER = ("dp_0", "dp_1", "dp_2", "owner")
MASK_ROWS = 8
TILE = 128


def upper_tiles(count):
    return [(i, j) for i in range(count) for j in range(i, count)]


def pack_kernel(at_ref, mask_ref, in_ref, grad_ref, out_ref, wide_ref, sem):
    layers, rows, width = in_ref.shape
    copies = []
    for s in range(layers):
        layer = at_ref[s]
        copies.append(
            pltpu.make_async_copy(in_ref.at[layer], out_ref.at[s, pl.ds(0, rows)], sem.at[s, 0])
        )
        copies.append(
            pltpu.make_async_copy(
                grad_ref.at[layer], out_ref.at[s, pl.ds(rows, rows)], sem.at[s, 1]
            )
        )
    for copy in copies:
        copy.start()
    wide_ref[...] = jnp.zeros(wide_ref.shape, wide_ref.dtype)
    for s in range(layers):
        line = mask_ref[pl.ds(at_ref[s], 1), :].astype(jnp.float32)
        wide_ref[s, :, :rows] = jnp.broadcast_to(line, (MASK_ROWS, rows)).astype(jnp.bfloat16)
    last = [
        pltpu.make_async_copy(
            wide_ref.at[s], out_ref.at[s, pl.ds(2 * rows, MASK_ROWS)], sem.at[s, 2]
        )
        for s in range(layers)
    ]
    for copy in last:
        copy.start()
    for copy in copies + last:
        copy.wait()


def pack(edge_in, edge_grad, row_mask, layer_at):
    layers, rows, width = edge_in.shape
    lines = 2 * rows + MASK_ROWS
    anywhere = pl.BlockSpec(memory_space=pl.ANY)
    return pl.pallas_call(
        pack_kernel,
        name="pack",
        out_shape=jax.ShapeDtypeStruct((layers, lines, width), jnp.bfloat16),
        in_specs=[
            pl.BlockSpec(memory_space=pltpu.SMEM),
            pl.BlockSpec(memory_space=pltpu.VMEM),
            anywhere,
            anywhere,
        ],
        out_specs=anywhere,
        scratch_shapes=[
            pltpu.VMEM((layers, MASK_ROWS, width), jnp.bfloat16),
            pltpu.SemaphoreType.DMA((layers, 3)),
        ],
    )(layer_at, row_mask, edge_in, edge_grad)


def half_tiles(count):
    upper = upper_tiles(count)
    half = count // 2
    return [
        [("in", i, j) for i, j in upper]
        + [("grad", i, j) for i in range(half) for j in range(count)],
        [("out", i, j) for i, j in upper]
        + [("grad", i, j) for i in range(half, count) for j in range(count)],
    ]


def half_lines(width):
    return len(half_tiles(width // TILE)[0]) * TILE


def gram_kernel(
    scale_factor, scale_grad, rows, core_ref, held_ref, mine_ref, theirs_ref,
    in_all, grad_all, mask_all, in_turned, grad_turned, accs, sem,
):
    sources = held_ref.shape[0]
    width = held_ref.shape[2]
    half = width // 2
    copies = []
    for k in range(sources):
        at = pl.ds(k * rows, rows)
        copies.append(
            [
                pltpu.make_async_copy(
                    held_ref.at[k, pl.ds(2 * rows, MASK_ROWS)], mask_all.at[k], sem.at[k, 2]
                ),
                pltpu.make_async_copy(held_ref.at[k, pl.ds(0, rows)], in_all.at[at], sem.at[k, 0]),
                pltpu.make_async_copy(
                    held_ref.at[k, pl.ds(rows, rows)], grad_all.at[at], sem.at[k, 1]
                ),
            ]
        )
    for group in copies:
        for copy in group:
            copy.start()
    for k, group in enumerate(copies):
        for copy in group:
            copy.wait()
        at = slice(k * rows, (k + 1) * rows)
        in_turned[:, at] = in_all[at, :].T
        grad_turned[:, at] = grad_all[at, :].T
    weights = jnp.concatenate([mask_all[k, :1, :rows] for k in range(sources)], axis=1)

    def dot(a, b):
        return jnp.dot(a, b, preferred_element_type=jnp.float32)

    accs[2] = dot(in_turned[...], grad_all[...])
    for n, turned, plain in ((0, in_turned, in_all), (1, grad_turned, grad_all)):
        kept = turned[...] * weights
        accs[n, :half, :] = dot(kept[:half], plain[...])
        accs[n, half:, half:] = dot(kept[half:], plain[:, half:])
    place = {"in": (0, scale_factor), "out": (1, scale_factor), "grad": (2, scale_grad)}
    halves = half_tiles(width // TILE)

    def write(ref, tiles):
        for spot, (kind, i, j) in enumerate(tiles):
            n, scale = place[kind]
            tile = accs[n, i * TILE : (i + 1) * TILE, j * TILE : (j + 1) * TILE] * scale
            ref[spot * TILE : (spot + 1) * TILE, :] = tile.astype(ref.dtype)

    for core in range(2):

        @pl.when(core_ref[0] == core)
        def _(core=core):
            write(mine_ref, halves[core])
            write(theirs_ref, halves[1 - core])


def gram(core, held, rows, width, rows_all):
    sources = held.shape[0]
    lines = half_lines(width)
    kernel = lambda *refs: gram_kernel(1.0 / rows_all, 1.0 / math.sqrt(rows_all), rows, *refs)
    inside = pl.BlockSpec(memory_space=pltpu.VMEM)
    return pl.pallas_call(
        kernel,
        name="gram",
        compiler_params=pltpu.CompilerParams(vmem_limit_bytes=28 << 20),
        out_shape=(
            jax.ShapeDtypeStruct((lines, TILE), jnp.float32),
            jax.ShapeDtypeStruct((lines, TILE), jnp.bfloat16),
        ),
        in_specs=[pl.BlockSpec(memory_space=pltpu.SMEM), pl.BlockSpec(memory_space=pl.ANY)],
        out_specs=(inside, inside),
        scratch_shapes=[
            pltpu.VMEM((sources * rows, width), jnp.bfloat16),
            pltpu.VMEM((sources * rows, width), jnp.bfloat16),
            pltpu.VMEM((sources, MASK_ROWS, width), jnp.bfloat16),
            pltpu.VMEM((width, sources * rows), jnp.bfloat16),
            pltpu.VMEM((width, sources * rows), jnp.bfloat16),
            pltpu.VMEM((3, width, width), jnp.float32),
            pltpu.SemaphoreType.DMA((sources, 3)),
        ],
    )(core, held)


def pair_kernel(mine_ref, other_ref, out_ref):
    out_ref[...] = (mine_ref[...] + other_ref[...].astype(jnp.float32)).astype(jnp.bfloat16)


def pair_sum(mine, other):
    inside = pl.BlockSpec(memory_space=pltpu.VMEM)
    return pl.pallas_call(
        pair_kernel,
        name="pair",
        compiler_params=pltpu.CompilerParams(vmem_limit_bytes=8 << 20),
        out_shape=jax.ShapeDtypeStruct(other.shape, other.dtype),
        in_specs=[inside, inside],
        out_specs=inside,
    )(mine, other)


def total_kernel(arrived_ref, copies_ref):
    whole = arrived_ref[0].astype(jnp.float32)
    for k in range(1, arrived_ref.shape[0]):
        whole += arrived_ref[k].astype(jnp.float32)
    low = whole.astype(jnp.bfloat16)
    for k in range(copies_ref.shape[0]):
        copies_ref[k] = low


def total_copies(arrived):
    return pl.pallas_call(
        total_kernel,
        name="total",
        compiler_params=pltpu.CompilerParams(vmem_limit_bytes=8 << 20),
        out_shape=jax.ShapeDtypeStruct(arrived.shape, arrived.dtype),
        in_specs=[pl.BlockSpec(memory_space=pltpu.VMEM)],
        out_specs=pl.BlockSpec(memory_space=pltpu.VMEM),
    )(arrived)


def newton_kernel(width, core_ref, own_ref, other_ref, out_ref, left_ref, right_ref, mid_ref):
    count = width // TILE
    halves = half_tiles(count)
    spots = {t: (h, k * TILE) for h in range(2) for k, t in enumerate(halves[h])}
    diagonal = (
        lax.broadcasted_iota(jnp.int32, (TILE, TILE), 0)
        == lax.broadcasted_iota(jnp.int32, (TILE, TILE), 1)
    )

    def unpack(h, ref):
        target = {"in": left_ref, "out": right_ref, "grad": mid_ref}
        for spot, (kind, i, j) in enumerate(halves[h]):
            tile = ref[spot * TILE : (spot + 1) * TILE, :].astype(jnp.float32)
            target[kind][i * TILE : (i + 1) * TILE, j * TILE : (j + 1) * TILE] = tile
            if kind != "grad" and i != j:
                target[kind][j * TILE : (j + 1) * TILE, i * TILE : (i + 1) * TILE] = tile.T

    for core in range(2):

        @pl.when(core_ref[0] == core)
        def _(core=core):
            unpack(core, own_ref)
            unpack(1 - core, other_ref)

    starts = []
    for ref in (left_ref, right_ref):
        trace = jnp.float32(0.0)
        for i in range(count):
            at = slice(i * TILE, (i + 1) * TILE)
            trace += jnp.sum(jnp.where(diagonal, ref[at, at], 0.0))
        shift = jnp.where(diagonal, trace * (0.05 / width), 0.0)
        for i in range(count):
            at = slice(i * TILE, (i + 1) * TILE)
            ref[at, at] += shift
        whole = ref[...]
        scale = lax.rsqrt(jnp.sum(whole * whole) + 1e-06)
        ref[...] = whole * scale
        starts.append(scale)

    def dot(a, b):
        return jnp.dot(a, b, preferred_element_type=jnp.float32)

    for step in range(ITERS):
        left = left_ref[...]
        right = right_ref[...]
        left_low = left.astype(jnp.bfloat16)
        right_low = right.astype(jnp.bfloat16)
        mid = mid_ref[...]
        mid = 2.0 * mid - dot(left_low, mid.astype(jnp.bfloat16))
        mid = 2.0 * mid - dot(mid.astype(jnp.bfloat16), right_low)
        if step < ITERS - 1:
            mid_ref[...] = mid
            left_ref[...] = 2.0 * left - dot(left_low, left_low)
            right_ref[...] = 2.0 * right - dot(right_low, right_low)
        else:
            out_ref[...] = (mid * starts[0] * starts[1]).astype(jnp.bfloat16)


def newton(core, own, other, width):
    inside = pl.BlockSpec(memory_space=pltpu.VMEM)
    return pl.pallas_call(
        lambda *refs: newton_kernel(width, *refs),
        name="newton",
        compiler_params=pltpu.CompilerParams(vmem_limit_bytes=16 << 20),
        out_shape=jax.ShapeDtypeStruct((width, width), jnp.bfloat16),
        in_specs=[pl.BlockSpec(memory_space=pltpu.SMEM), inside, inside],
        out_specs=inside,
        scratch_shapes=[pltpu.VMEM((width, width), jnp.float32)] * 3,
    )(core, own, other)


def local(edge_in, edge_grad, row_mask, layer_at):
    rows = edge_in.shape[1]
    width = edge_in.shape[2]
    far, pair = DP[:2], DP[2]
    replicas = lax.axis_size(far)
    rows_all = rows * lax.axis_size(DP) * lax.axis_size("owner")
    swap = [(0, 1), (1, 0)]
    core = lax.axis_index(pair).astype(jnp.int32).reshape(1)
    sent = pack(edge_in, edge_grad, row_mask, layer_at)
    held = lax.all_to_all(sent, "owner", 0, 0, tiled=True)
    mine, theirs = gram(core, held, rows, width, rows_all)
    pieces = pair_sum(mine, lax.ppermute(theirs, pair, swap)).reshape(replicas, -1, TILE)
    arrived = lax.all_to_all(pieces, far, 0, 0, tiled=True)
    own = lax.all_to_all(total_copies(arrived), far, 0, 0, tiled=True).reshape(-1, TILE)
    update = newton(core, own, lax.ppermute(own, pair, swap), width)
    return update[None]


def solution(mesh):
    split = Mesh(
        mesh.devices.reshape(8, 2, 2, mesh.shape["owner"]), ("dp_0", "dp_1", "dp_2", "owner")
    )
    placed = (P(None, DP_OWNER, None), P(None, DP_OWNER, None), P(None, DP_OWNER), P())
    return jax.shard_map(
        local, mesh=split, in_specs=placed, out_specs=P("owner", None, None), check_vma=False
    )
```

time: 165 us -> 256 us (1.55)
  Pallas kernels: 24.5 us -> 141 us
  blocking collectives: 140 us -> 52.5 us
  waiting for transfers between devices: 0 us -> 52.7 us
  starting transfers between devices: 0 us -> 9.58 us
    pallas_call x3 -> x4, Pallas kernels: 17.4 us -> 135 us  [the longest x1 129 us: pack(): pl.pallas_call(pack_kernel, name='pack', out_shape=jax.ShapeDtypeStruct((...]
    all_to_all x3 -> x2, blocking collectives: 140 us -> 52.5 us  [the longest x1 30.6 us: local(): arrived = lax.all_to_all(pieces, far, 0, 0, tiled=True)]
    all_to_all x0 -> x1, waiting for transfers between devices: none -> 49.5 us  [local(): held = lax.all_to_all(sent, 'owner', 0, 0, tiled=True)]
    all_to_all x0 -> x1, starting transfers between devices: none -> 5.95 us  [local(): held = lax.all_to_all(sent, 'owner', 0, 0, tiled=True)]
    ppermute x0 -> x2, starting transfers between devices: none -> 3.64 us  [the longest x1 2.78 us: local(): update = newton(core, own, lax.ppermute(own, pair, swap), width)]
    ppermute x0 -> x2, waiting for transfers between devices: none -> 3.26 us  [the longest x1 1.63 us: local(): lax.ppermute(theirs, pair, swap)]
  transfers between devices with their start and end apart: 0 -> 3, of which waited for: 0 -> 3; matrix products, arithmetic and copies ran while one was open for 0% -> 0% of each run, Pallas kernels for 0% -> 0%
where the time goes in v1:
time: 256 us
  Pallas kernels  141 us (55%)
  waiting for transfers between devices  52.7 us (21%)
  blocking collectives  52.5 us (21%)
  starting transfers between devices  9.58 us (4%)
    pallas_call x1, Pallas kernels, pack(): pl.pallas_call(pack_kernel, name='pack', out_shape=jax.ShapeDtypeStruct((...  129 us
    all_to_all x1, waiting for transfers between devices, local(): held = lax.all_to_all(sent, 'owner', 0, 0, tiled=True)  49.5 us
    all_to_all x1, blocking collectives, local(): arrived = lax.all_to_all(pieces, far, 0, 0, tiled=True)  30.6 us
    all_to_all x1, blocking collectives, local(): lax.all_to_all(total_copies(arrived), far, 0, 0, tiled=True)  21.9 us
    pallas_call x1, Pallas kernels, newton(): pl.pallas_call(lambda *refs: newton_kernel(width, *refs), name='newton',...  6.03 us
    all_to_all x1, starting transfers between devices, local(): held = lax.all_to_all(sent, 'owner', 0, 0, tiled=True)  5.95 us
    pallas_call x1, Pallas kernels, gram(): pl.pallas_call(kernel, name='gram', compiler_params=pltpu.CompilerParams(...  5.61 us
  transfers between devices with their start and end apart: 3, of which 3 were waited for; matrix products, arithmetic and copies ran while one was open for 0% of the time, Pallas kernels for 0%

profile of v1, /device:TPU:1, one launch (start us, length us, event | category | flops | bytes accessed | tf_op | source)
XLA Modules:
  0.0 255.7 jit_solution(106655871895054089)
XLA Ops:
  0.0 129.1 %pack.1 = bf16[8,520,512]{2,1,0:T(8,128)(2,1)} custom-call(s32[8]{0:T(128)} %at_ref.1, s32[8,256]{1,0:T(8,128)} %mask_ref.1, bf16[8,256,512]{2,1,0:T(8,128)(2,1)} %in_ref.1, bf16[8,256,512]{2,1,0:T(8,128)(2,1)} %grad_ref.1), custom_call_target="tpu_custom_call" | custom-call | tf_op jit(solution)/shard_map/pack/pallas_call | solution.py:57
  129.1 5.9 %all-to-all-start = ((bf16[8,520,512]{2,1,0:T(8,128)(2,1)}), bf16[8,520,512]{2,1,0:T(8,128)(2,1)}, u32[]{:S(2)}, u32[]{:S(2)}) async-start(bf16[8,520,512]{2,1,0:T(8,128)(2,1)} %pack.1), calls=%async_computation | async-start | bytes 8519680 | tf_op jit(solution)/shard_map/all_to_all | solution.py:290
  135.0 49.5 %all-to-all-done.refs_1_ = bf16[8,520,512]{2,1,0:T(8,128)(2,1)} async-done(((bf16[8,520,512]{2,1,0:T(8,128)(2,1)}), bf16[8,520,512]{2,1,0:T(8,128)(2,1)}, u32[]{:S(2)}, u32[]{:S(2)}) %all-to-all-start) | async-done | bytes 4259872 | tf_op jit(solution)/shard_map/all_to_all | solution.py:290
  184.5 5.6 %gram.1 = (f32[2304,128]{1,0:T(8,128)S(1)}, bf16[2304,128]{1,0:T(8,128)(2,1)S(1)}) custom-call(s32[1]{0:T(128)} %bitcast.refs_0_, bf16[8,520,512]{2,1,0:T(8,128)(2,1)} %all-to-all-done.refs_1_), custom_call_target="tpu_custom_call" | custom-call | tf_op jit(solution)/shard_map/gram/pallas_call | solution.py:152
  190.2 0.9 collective-permute-start
  191.0 1.6 collective-permute-done.other_ref
  192.6 0.1 pair.1
  192.7 30.6 %all_to_all.15.arrived_ref = bf16[16,144,128]{2,1,0:T(8,128)(2,1)S(1)} all-to-all(bf16[16,144,128]{2,1,0:T(8,128)(2,1)S(1)} %bitcast.6), channel_id=1, replica_groups=mesh['dp_0'=8,'dp_1'=2,'dp_2'=2,'owner'=8] {'dp_0','dp_1'}, dimensions={0} | all-to-all | bytes 1179648 | tf_op jit(solution)/shard_map/all_to_all | solution.py:293
  223.4 0.1 total.1
  223.4 21.9 %all_to_all.16 = bf16[16,144,128]{2,1,0:T(8,128)(2,1)S(1)} all-to-all(bf16[16,144,128]{2,1,0:T(8,128)(2,1)S(1)} %total.1), channel_id=1, replica_groups=mesh['dp_0'=8,'dp_1'=2,'dp_2'=2,'owner'=8] {'dp_0','dp_1'}, dimensions={0} | all-to-all | bytes 1179648 | tf_op jit(solution)/shard_map/all_to_all | solution.py:294
  245.3 2.8 %collective-permute-start.1 = (bf16[2304,128]{1,0:T(8,128)(2,1)S(1)}, bf16[2304,128]{1,0:T(8,128)(2,1)S(1)}, u32[]{:S(2)}, u32[]{:S(2)}) collective-permute-start(bf16[2304,128]{1,0:T(8,128)(2,1)S(1)} %bitcast.4), channel_id=1, source_target_pairs={{0,8},{8,0},{1,9},{9,1},{2,10},{10,2},{3,11},{11,3},{4,12},{12,4},... | collective-permute-start | bytes 1769480 | tf_op jit(solution)/shard_map/ppermute | solution.py:295
  248.1 1.6 collective-permute-done.1.refs_2_
  249.7 6.0 %newton.1 = bf16[512,512]{1,0:T(8,128)(2,1)} custom-call(s32[1]{0:T(128)} %bitcast.refs_0_, bf16[2304,128]{1,0:T(8,128)(2,1)S(1)} %bitcast.5, bf16[2304,128]{1,0:T(8,128)(2,1)S(1)} %collective-permute-done.1.refs_2_), custom_call_target="tpu_custom_call" | custom-call | tf_op jit(solution)/shard_map/newton/pallas_call | solution.py:270
Async XLA Ops:
  129.1 55.4 %all-to-all-start = ((bf16[8,520,512]{2,1,0:T(8,128)(2,1)}), bf16[8,520,512]{2,1,0:T(8,128)(2,1)}, u32[]{:S(2)}, u32[]{:S(2)}) async-start(bf16[8,520,512]{2,1,0:T(8,128)(2,1)} %pack.1), calls=%async_computation | async-start | bytes 8519680 | tf_op jit(solution)/shard_map/all_to_all | solution.py:290
  190.2 2.5 collective-permute-start
  245.3 4.4 %collective-permute-start.1 = (bf16[2304,128]{1,0:T(8,128)(2,1)S(1)}, bf16[2304,128]{1,0:T(8,128)(2,1)S(1)}, u32[]{:S(2)}, u32[]{:S(2)}) collective-permute-start(bf16[2304,128]{1,0:T(8,128)(2,1)S(1)} %bitcast.4), channel_id=1, source_target_pairs={{0,8},{8,0},{1,9},{9,1},{2,10},{10,2},{3,11},{11,3},{4,12},{12,4},... | collective-permute-start | bytes 1769480 | tf_op jit(solution)/shard_map/ppermute | solution.py:295
